TPU v7x, 32 devices: a whole 2x2x4 slice. The times are simulated.
32 devices in a mesh: grp: 2 (over y), seq: 16 (over z, x, core).
Axes of the slice: x: 2, y: 2, z: 4, core: 2. Of those that a mesh axis runs over, the one named last changes fastest.
Arguments:
- queries: bfloat16 [4096, 12288], P(('grp', 'seq')), parts along dimension 0, may hold values from -8 to 8
- sum_keys: bfloat16 [256, 768], P(('grp', 'seq')), parts along dimension 0, may hold values from -4 to 4
- sum_values: bfloat16 [256, 512], P(('grp', 'seq')), parts along dimension 0, may hold values from -24 to 24
- limits: int32 [64], P('grp'), parts along dimension 0, may hold values from 1 to 128, as said below
- valid_tokens: int32 [2], P('grp'), parts along dimension 0, may hold values from 1024 to 2048
Outputs:
- attended: bfloat16 [4096, 8192], P(('grp', 'seq')), parts along dimension 0
There are 2 independent parts, one for each index of `grp`. A program takes and returns all parts, laid end to end along the dimension named above; each array names one. Nothing has to cross between parts.
Inputs may be any that keep to these rules, and one draw needn't show every extreme that they name: limits[b] is at least 1 and at most max(1, (64 * b - 32) // 16 + 1), the number of summaries that end at or before the block's first token; the last block reaches this bound.
All inputs are finite; a program needn't handle non-finite values.
Results may differ from a plain program's by a relative error of at most 0.0027.
Values may be sent and summed in bfloat16 or wider, within the bound.
No kernel may reach another device: no remote copies, remote signals or barrier semaphores. Data moves between devices by JAX's collectives and lax.ppermute only.
A program may use at most 64 MiB of HBM per device.

v0:
```python
import jax
import jax.numpy as jnp
from jax import lax
from jax.sharding import PartitionSpec as P

H = 64
G = 4
DK = 192
DV = 128
STRIDE = 16
CBLOCK = 32
QB = 64


def per_device(queries, sum_keys, sum_values, limits, valid_tokens):
    tok_rows = queries.shape[0]
    per_group = H // G
    inv_root = float(DK) ** (-0.5)
    usable = jnp.maximum((valid_tokens[0] - CBLOCK) // STRIDE + 1, 1)
    my_index = lax.axis_index("seq")
    block_count = tok_rows // QB
    local_blocks = jnp.arange(block_count, dtype=jnp.int32)
    block_ids = my_index * block_count + local_blocks
    table_ids = jnp.arange(limits.shape[0], dtype=jnp.int32)
    block_limits = jnp.sum(
        jnp.where(table_ids[None, :] == block_ids[:, None], limits[None, :], 0), axis=1
    )
    row_caps = jnp.repeat(jnp.minimum(block_limits, usable), QB)
    highest = jnp.max(row_caps)
    grouped = queries.reshape(tok_rows, G, per_group, DK)
    all_keys, all_values = (
        lax.all_gather(sum_keys, "seq", axis=0, tiled=True),
        lax.all_gather(sum_values, "seq", axis=0, tiled=True),
    )
    total = all_keys.shape[0]
    step_len = min(512, total)
    step_count = total // step_len

    def fold_block(block_pos, state_now):
        first_id = block_pos * step_len

        def update(current):
            run_max, run_sum, run_out = current
            key_block = lax.dynamic_slice_in_dim(all_keys, first_id, step_len, 0).reshape(
                step_len, G, DK
            )
            value_block = lax.dynamic_slice_in_dim(all_values, first_id, step_len, 0).reshape(
                step_len, G, DV
            )
            scores = (
                jnp.einsum("tgjd,sgd->tgjs", grouped, key_block, preferred_element_type=jnp.float32)
                * inv_root
            )
            summary_ids = first_id + jnp.arange(step_len, dtype=jnp.int32)
            visible = (summary_ids[None, :] < row_caps[:, None])[:, None, None, :]
            scores = jnp.where(visible, scores, -1e30)
            new_max = jnp.maximum(run_max, jnp.max(scores, axis=-1))
            rescale = jnp.exp(run_max - new_max)
            weights = jnp.where(visible, jnp.exp(scores - new_max[..., None]), 0.0)
            new_sum = run_sum * rescale + jnp.sum(weights, axis=-1)
            added = jnp.einsum(
                "tgjs,sgd->tgjd",
                weights.astype(jnp.bfloat16),
                value_block,
                preferred_element_type=jnp.float32,
            )
            return (new_max, new_sum, run_out * rescale[..., None] + added)

        def unchanged(current):
            return current

        return lax.cond(first_id < highest, update, unchanged, state_now)

    start_state = (
        jnp.full((tok_rows, G, per_group), -1e30, jnp.float32),
        jnp.zeros((tok_rows, G, per_group), jnp.float32),
        jnp.zeros((tok_rows, G, per_group, DV), jnp.float32),
    )
    run_max, run_sum, run_out = lax.fori_loop(0, step_count, fold_block, start_state)
    attended = (run_out / run_sum[..., None]).reshape(tok_rows, H * DV).astype(jnp.bfloat16)
    return attended


def solution(mesh):
    placed = (
        P(("grp", "seq"), None),
        P(("grp", "seq"), None),
        P(("grp", "seq"), None),
        P("grp"),
        P("grp"),
    )
    return jax.shard_map(
        per_device, mesh=mesh, in_specs=placed, out_specs=P(("grp", "seq"), None), check_vma=False
    )
```

profile of v0, /device:TPU:0, one launch (start us, length us, event | category | flops | bytes accessed | tf_op | source)
XLA Modules:
  0.0 68.0 jit_solution(9087807829274325061)
XLA Ops:
  0.7 0.8 %fusion.13 = s32[2]{0:T(128)S(1)} fusion(s32[32]{0:T(128)} %param.10, s32[2]{0:T(128)S(1)} %iota_add_fusion), kind=kLoop, calls=%fused_computation.22 | loop fusion | flops 190 | bytes 144 | tf_op jit(solution)/shard_map/reduce_sum | solution.py:25
  1.5 0.7 %broadcast_reduce_fusion = s32[]{:T(128)} fusion(s32[2]{0:T(128)S(1)} %broadcast_minimum_fusion), kind=kLoop, calls=%fused_computation.24 | loop fusion | flops 127 | bytes 12 | tf_op jit(solution)/shard_map/reduce_max | solution.py:29
  2.9 0.1 broadcast_in_dim.62
  3.0 23.7 %all_gather.7 = bf16[128,512]{1,0:T(8,128)(2,1)S(1)} all-gather(bf16[8,512]{1,0:T(8,128)(2,1)} %param.9), channel_id=1, replica_groups=mesh['grp'=2,'seq'=16] {'seq'}, dimensions={0}, use_global_device_ids=true | all-gather | bytes 139264 | tf_op jit(solution)/shard_map/all_gather | solution.py:33
  26.6 18.2 %all_gather.6 = bf16[128,768]{1,0:T(8,128)(2,1)S(1)} all-gather(bf16[8,768]{1,0:T(8,128)(2,1)} %param.8), channel_id=1, replica_groups=mesh['grp'=2,'seq'=16] {'seq'}, dimensions={0}, use_global_device_ids=true | all-gather | bytes 208896 | tf_op jit(solution)/shard_map/all_gather | solution.py:32
  44.8 0.6 broadcast_in_dim.63
  45.4 2.4 %broadcast_in_dim.64 = f32[128,4,16,128]{3,0,2,1:T(8,128)} broadcast(f32[]{:T(128)} %constant.59.clone.1), dimensions={} | broadcast | bytes 4194308 | tf_op jit(solution)/shard_map/broadcast_in_dim | solution.py:77
  47.9 12.8 %conditional.1 = ((f32[128,4,16]{0,2,1:T(8,128)}, f32[128,4,16,128]{3,0,2,1:T(8,128)})) conditional(s32[]{:T(128)} %convert_element_type.15, (f32[128,4,16]{0,2,1:T(8,128)}, f32[128,4,16,128]{3,0,2,1:T(8,128)}) %tuple.22, (s32[2,64]{1,0:T(2,128)S(1)}, bf16[128,768]{1,0:T(8,128)(2,1)S(1)}, bf16[128,12288]{1,0:T(8,128)(2,1)}, f32[128,4,16]{0,2,1:T(8,128)}, ...), branch_computations={%region_2.3_spmd, %region_3.0_spmd} | conditional | flops 686858240 | bytes 65930860 | solution.py:72
  47.9 0.7 %reshape.61 = bf16[128,4,128]{2,1,0:T(4,128)(2,1)} reshape(bf16[128,512]{1,0:T(8,128)(2,1)S(1)} %get-tuple-element.91) | data formatting | bytes 262144 | tf_op jit(solution)/shard_map/while/body/eval_jaxpr/cond/branch_1_fun/reshape | solution.py:47
  48.6 0.1 lt.24
  48.7 0.2 copy.19
  48.8 3.5 %copy.20 = bf16[128,12288]{0,1:T(8,128)(2,1)S(1)} copy(bf16[128,12288]{1,0:T(8,128)(2,1)} %get-tuple-element.112) | data formatting | bytes 6291456 | tf_op jit(solution)/shard_map
  52.3 0.9 %fusion = (f32[128,4,16]{0,2,1:T(8,128)S(1)}, f32[4,128,128,16]{2,1,3,0:T(8,128)S(1)}) fusion(pred[128,128]{0,1:T(8,128)(4,1)S(1)} %iota_compare_fusion, bf16[128,4,192,1]{0,2,3,1:T(8,128)(2,1)S(1)} %bitcast.30, bf16[128,4,16,192]{0,3,2,1:T(8,128)(2,1)S(1)} %bitcast.28), kind=kOutput, calls=%fused_computation.3 | convolution fusion | flops 405790720 | bytes 7585792 | tf_op jit(solution)/shard_map/while/body/eval_jaxpr/cond/branch_1_fun/tgjd,sgd->tgjs/dot_general | solution.py:51
  53.2 0.0 copy-start
  53.2 0.0 copy-start.2
  53.3 1.2 %fusion.2 = f32[128,4,16]{0,2,1:T(8,128)S(1)} fusion(f32[4,128,128,16]{2,1,3,0:T(8,128)S(1)} %get-tuple-element.119, f32[128,4,16]{0,2,1:T(8,128)S(1)} %broadcast_maximum_fusion, pred[128,128]{0,1:T(8,128)(4,1)S(1)} %iota_compare_fusion), kind=kLoop, calls=%fused_computation.5 | loop fusion | flops 5234688 | bytes 4276224 | tf_op jit(solution)/shard_map/while/body/eval_jaxpr/cond/branch_1_fun/reduce_sum | solution.py:60
  54.5 1.4 %subtract_exponential_fusion = (f32[128,4,16]{0,2,1:T(8,128)S(1)}, f32[128,4,16]{0,2,1:T(8,128)}) fusion(f32[128,4,16]{0,2,1:T(8,128)S(1)} %get-tuple-element.118, f32[128,4,16]{0,2,1:T(8,128)S(1)} %fusion.2, f32[128,4,16]{0,2,1:T(8,128)} %get-tuple-element.86), kind=kLoop, calls=%fused_computation.14 | loop fusion | flops 32768 | bytes 163840 | tf_op jit(solution)/shard_map/while/body/eval_jaxpr/cond/branch_1_fun/exp | solution.py:58
  55.9 0.0 copy-done
  55.9 0.0 copy-done.2
  55.9 2.8 %bitcast_add_fusion = f32[128,4,16,128]{3,0,2,1:T(8,128)S(1)} fusion(f32[128,4,16,128]{3,0,2,1:T(8,128)S(1)} %copy-done, f32[4,128,128,16]{2,1,3,0:T(8,128)S(1)} %get-tuple-element.119, f32[128,4,16]{0,2,1:T(8,128)S(1)} %get-tuple-element.116, f32[128,4,16]{0,2,1:T(8,128)S(1)} %broadcast_maximum_fusion, pred[128,128]{0,1:T(8,128)(4,1)S(1)} %iota_compare_fusion, ...), kind=kOutput, calls=%fused_computation | convolution fusion | flops 275775488 | bytes 12795904 | tf_op jit(solution)/shard_map/while/body/eval_jaxpr/cond/branch_1_fun/tgjs,sgd->tgjd/dot_general | solution.py:61
  58.7 0.0 copy-start.1
  58.7 1.9 %copy-done.1 = f32[128,4,16,128]{3,0,2,1:T(8,128)} copy-done((f32[128,4,16,128]{3,0,2,1:T(8,128)}, f32[128,4,16,128]{3,0,2,1:T(8,128)S(1)}, u32[]{:S(2)}) %copy-start.1) | copy-done | bytes 4194328 | tf_op jit(solution)/shard_map/while/body/eval_jaxpr/cond
  60.6 2.9 %divide_convert_fusion = bf16[128,4,16,128]{3,0,2,1:T(8,128)(2,1)S(1)} fusion(f32[128,4,16,128]{3,0,2,1:T(8,128)} %get-tuple-element.94, f32[128,4,16]{0,2,1:T(8,128)} %get-tuple-element.95), kind=kLoop, calls=%fused_computation.19 | loop fusion | flops 2097152 | bytes 6324224 | tf_op jit(solution)/shard_map/convert_element_type | solution.py:80
  63.5 1.4 %copy.21 = bf16[128,4,16,128]{3,2,1,0:T(8,128)(2,1)S(1)} copy(bf16[128,4,16,128]{3,0,2,1:T(8,128)(2,1)S(1)} %divide_convert_fusion) | data formatting | bytes 4194304 | tf_op jit(solution)/shard_map/convert_element_type | solution.py:80
  64.9 3.1 %copy.31 = bf16[16,8,64,128]{3,1,2,0:T(8,128)(2,1)} copy(bf16[16,8,64,128]{3,2,1,0:T(8,128)(2,1)S(1)} %bitcast.29) | data formatting | bytes 4194304
  (4 shorter events, 0.0 us)
Async XLA Ops:
  53.2 2.7 %copy-start = (f32[128,4,16,128]{3,0,2,1:T(8,128)S(1)}, f32[128,4,16,128]{3,0,2,1:T(8,128)}, u32[]{:S(2)}) copy-start(f32[128,4,16,128]{3,0,2,1:T(8,128)} %get-tuple-element.90) | copy-start | bytes 12582916 | tf_op jit(solution)/shard_map/while/body/eval_jaxpr/cond
  53.2 2.7 %copy-start.2 = (bf16[128,4,128]{2,1,0:T(4,128)(2,1)S(1)}, bf16[128,4,128]{2,1,0:T(4,128)(2,1)}, u32[]{:S(2)}) copy-start(bf16[128,4,128]{2,1,0:T(4,128)(2,1)} %reshape.61) | copy-start | bytes 393220 | tf_op jit(solution)/shard_map/while/body/eval_jaxpr/cond
  58.7 1.9 %copy-start.1 = (f32[128,4,16,128]{3,0,2,1:T(8,128)}, f32[128,4,16,128]{3,0,2,1:T(8,128)S(1)}, u32[]{:S(2)}) copy-start(f32[128,4,16,128]{3,0,2,1:T(8,128)S(1)} %bitcast_add_fusion) | copy-start | bytes 12582916 | tf_op jit(solution)/shard_map/while/body/eval_jaxpr/cond
where the time goes:
time: 68.2 us; the launch traced here: 68 us
  blocking collectives  41.9 us (61%)
  local copies, waits for them, and re-layouts  13.9 us (20%)
  other arithmetic  7.09 us (10%)
  matrix products  3.69 us (5%)
  between operations  1.36 us (2%)
    all_gather x1, blocking collectives, per_device(): lax.all_gather(sum_values, 'seq', axis=0, tiled=True)  23.7 us
    all_gather x1, blocking collectives, per_device(): lax.all_gather(sum_keys, 'seq', axis=0, tiled=True)  18.2 us
    another operation x2, local copies, waits for them, and re-layouts  3.64 us
    unnamed x1, local copies, waits for them, and re-layouts  3.12 us
    convert_element_type x1, other arithmetic, per_device(): (run_out / run_sum[..., None]).reshape(tok_rows, H * DV)  2.88 us
    dot_general x1, matrix products, update(): jnp.einsum('tgjs,sgd->tgjd', weights.astype(jnp.bfloat16), value_block, p...  2.79 us
    broadcast_in_dim x1, local copies, waits for them, and re-layouts, per_device(): jnp.zeros((tok_rows, G, per_group, DV), jnp.float32)  2.44 us
    cond x6, local copies, waits for them, and re-layouts  1.93 us

commit v1 on v0

v1 whole, which is shorter than its diff:
```python
import functools
import math

import jax
import jax.numpy as jnp
from jax import lax
from jax.experimental import pallas as pl
from jax.experimental.pallas import tpu as pltpu
from jax.sharding import PartitionSpec as P

H = 64
G = 4
DK = 192
DV = 128
STRIDE = 16
CBLOCK = 32
QB = 64
PER = H // G
HIDDEN = -1e30


def exchange_masks(count):
    bits = count.bit_length() - 1
    return [(1 << b) | 1 for b in range(bits - 1, 0, -1)] + [1]


def gather_parts(x, count):
    if count < 2 or count & (count - 1) or x.shape[0] & (x.shape[0] - 1):
        whole = lax.all_gather(x, "seq", axis=0, tiled=True)
        return [whole], None
    masks = exchange_masks(count)
    for mask in masks[:-1]:
        other = lax.ppermute(x, "seq", [(i, i ^ mask) for i in range(count)])
        x = jnp.concatenate([x, other], axis=0)
    other = lax.ppermute(x, "seq", [(i, i ^ masks[-1]) for i in range(count)])
    return [x, other], masks


def attend(masks, shard, parts, *refs):
    q_ref, *kv_refs = refs[: 1 + parts]
    limits_ref, valid_ref, out_ref, o_ref, sem = refs[1 + parts :]
    tokens = q_ref.shape[0]
    total = sum(r.shape[0] for r in kv_refs)
    blocks = tokens // QB
    me = lax.axis_index("seq")
    usable = jnp.maximum(((valid_ref[0] - CBLOCK) >> (STRIDE.bit_length() - 1)) + 1, 1)
    lane = lax.broadcasted_iota(jnp.int32, (8, total), 1)
    if masks is None:
        ids = lane
    else:
        low = shard.bit_length() - 1
        owner = jnp.full_like(lane, me)
        for bit, mask in enumerate(masks):
            owner = owner ^ (((lane >> (low + bit)) & 1) * mask)
        ids = owner * shard + (lane & (shard - 1))
    biases = [
        jnp.where(ids < jnp.minimum(limits_ref[me * blocks + b], usable), 0.0, HIDDEN)[:1]
        for b in range(blocks)
    ]
    factor = math.log2(math.e) * float(DK) ** -0.5
    wide = 2 * DV
    col = lax.broadcasted_iota(jnp.int32, (total, wide), 1)

    def keys_at(g, offset):
        start = g * DK
        base = start // 128 * 128
        window = jnp.concatenate([r[:, base : base + wide] for r in kv_refs], axis=0).astype(jnp.float32)
        shift = (offset - (start - base)) % wide
        if shift:
            window = pltpu.roll(window, shift, 1)
        return jnp.where((col >= offset) & (col < offset + DK), window, 0.0).astype(jnp.bfloat16)

    pairs = PER // 2
    copies = []
    for g in range(G):
        v_start = G * DK + g * DV
        values = jnp.concatenate([r[:, v_start : v_start + DV] for r in kv_refs], axis=0)
        sides = []
        for side in range(2):
            weights = keys_at(g, side * (wide - DK))
            q0 = g * PER * DK + side * 128
            rows = jnp.concatenate(
                [q_ref[:, q0 + j * 2 * DK : q0 + j * 2 * DK + wide] for j in range(pairs)], axis=0
            )
            scores = lax.dot_general(
                rows, weights, (((1,), (1,)), ((), ())), preferred_element_type=jnp.float32
            )
            scores = scores.reshape(pairs, blocks, QB, total)
            scores = jnp.concatenate([scores[:, b : b + 1] + biases[b] for b in range(blocks)], axis=1)
            scores = scores.reshape(pairs * tokens, total)
            top = jnp.max(scores, axis=1, keepdims=True)
            w = jnp.exp2((scores - top) * factor)
            norm = jnp.sum(w, axis=1, keepdims=True)
            sides.append((w.astype(jnp.bfloat16), 1.0 / norm))
        (wa, ra), (wb, rb) = sides
        if total <= 128:
            zeros = jnp.zeros_like(values)
            both = jnp.concatenate(
                [jnp.concatenate([values, zeros], axis=1), jnp.concatenate([zeros, values], axis=1)], axis=0
            )
            out = jnp.dot(jnp.concatenate([wa, wb], axis=1), both, preferred_element_type=jnp.float32)
            outa, outb = out[:, :DV], out[:, DV:]
        else:
            outa = jnp.dot(wa, values, preferred_element_type=jnp.float32)
            outb = jnp.dot(wb, values, preferred_element_type=jnp.float32)
        outa = (outa * ra).astype(jnp.bfloat16)
        outb = (outb * rb).astype(jnp.bfloat16)
        for j in range(pairs):
            at = (g * PER + 2 * j) * DV
            o_ref[:, at : at + DV] = outa[j * tokens : (j + 1) * tokens]
            o_ref[:, at + DV : at + 2 * DV] = outb[j * tokens : (j + 1) * tokens]
        span = pl.ds(g * PER * DV, PER * DV)
        copy = pltpu.make_async_copy(o_ref.at[:, span], out_ref.at[:, span], sem.at[g])
        copy.start()
        copies.append(copy)
    for copy in copies:
        copy.wait()


def per_device(count, queries, sum_keys, sum_values, limits, valid_tokens):
    tokens = queries.shape[0]
    shard = sum_keys.shape[0]
    halves, masks = gather_parts(jnp.concatenate([sum_keys, sum_values], axis=1), count)
    vmem = pl.BlockSpec(memory_space=pltpu.VMEM)
    smem = pl.BlockSpec(memory_space=pltpu.SMEM)
    return pl.pallas_call(
        functools.partial(attend, masks, shard, len(halves)),
        out_shape=jax.ShapeDtypeStruct((tokens, H * DV), jnp.bfloat16),
        in_specs=[vmem] * (1 + len(halves)) + [smem, smem],
        out_specs=pl.BlockSpec(memory_space=pl.ANY),
        scratch_shapes=[pltpu.VMEM((tokens, H * DV), jnp.bfloat16), pltpu.SemaphoreType.DMA((G,))],
        compiler_params=pltpu.CompilerParams(vmem_limit_bytes=40 * 1024 * 1024),
    )(queries, *halves, limits, valid_tokens)


def solution(mesh):
    placed = (
        P(("grp", "seq"), None),
        P(("grp", "seq"), None),
        P(("grp", "seq"), None),
        P("grp"),
        P("grp"),
    )
    return jax.shard_map(
        functools.partial(per_device, mesh.shape["seq"]),
        mesh=mesh,
        in_specs=placed,
        out_specs=P(("grp", "seq"), None),
        check_vma=False,
    )
```

time: 68.2 us -> 23.4 us (0.34)
  blocking collectives: 41.9 us -> 0 us
  local copies, waits for them, and re-layouts: 13.9 us -> 3.95 us
  starting transfers between devices: 0 us -> 7.51 us
  other arithmetic: 7.09 us -> 0.02 us
  waiting for transfers between devices: 0 us -> 6.21 us
  Pallas kernels: 0 us -> 4.66 us
  matrix products: 3.69 us -> 0 us
  between operations: 1.36 us -> 0.66 us
    all_gather x2 -> x0, blocking collectives: 41.9 us -> none  [the longest x1 23.7 us: per_device(): lax.all_gather(sum_values, 'seq', axis=0, tiled=True)]
    ppermute x0 -> x4, starting transfers between devices: none -> 7.51 us  [the longest x3 7.16 us: gather_parts(): other = lax.ppermute(x, 'seq', [(i, i ^ mask) for i in range(count)])]
    ppermute x0 -> x4, waiting for transfers between devices: none -> 6.21 us  [the longest x3 5.74 us: gather_parts(): other = lax.ppermute(x, 'seq', [(i, i ^ mask) for i in range(count)])]
    pallas_call x0 -> x1, Pallas kernels: none -> 4.66 us  [per_device(): pl.pallas_call(functools.partial(attend, masks, shard, len(halves)), out_...]
    dot_general x2 -> x0, matrix products: 3.69 us -> none  [the longest x1 2.79 us: update(): jnp.einsum('tgjs,sgd->tgjd', weights.astype(jnp.bfloat16), value_block, p...]
    another operation x2 -> x0, local copies, waits for them, and re-layouts: 3.64 us -> none
    broadcast_in_dim x3 -> x0, local copies, waits for them, and re-layouts: 3.11 us -> none  [the longest x1 2.44 us: per_device(): jnp.zeros((tok_rows, G, per_group, DV), jnp.float32)]
    convert_element_type x1 -> x0, other arithmetic: 2.88 us -> none  [per_device(): (run_out / run_sum[..., None]).reshape(tok_rows, H * DV)]
  transfers between devices with their start and end apart: 0 -> 4, of which waited for: 0 -> 4; matrix products, arithmetic and copies ran while one was open for 0% -> 0% of each run, Pallas kernels for 0% -> 0%
where the time goes in v1:
time: 23.4 us; the launch traced here: 23 us
  starting transfers between devices  7.51 us (32%)
  waiting for transfers between devices  6.21 us (27%)
  Pallas kernels  4.66 us (20%)
  local copies, waits for them, and re-layouts  3.95 us (17%)
  between operations  0.66 us (3%)
    ppermute x3, starting transfers between devices, gather_parts(): other = lax.ppermute(x, 'seq', [(i, i ^ mask) for i in range(count)])  7.16 us
    ppermute x3, waiting for transfers between devices, gather_parts(): other = lax.ppermute(x, 'seq', [(i, i ^ mask) for i in range(count)])  5.74 us
    pallas_call x1, Pallas kernels, per_device(): pl.pallas_call(functools.partial(attend, masks, shard, len(halves)), out_...  4.66 us
    unnamed x5, local copies, waits for them, and re-layouts  3.25 us
    concatenate x1, local copies, waits for them, and re-layouts, per_device(): jnp.concatenate([sum_keys, sum_values], axis=1)  0.7 us
  transfers between devices with their start and end apart: 4, of which 4 were waited for; matrix products, arithmetic and copies ran while one was open for 0% of the time, Pallas kernels for 0%

profile of v1, /device:TPU:0, one launch (start us, length us, event | category | flops | bytes accessed | tf_op | source)
XLA Modules:
  0.0 23.0 jit_solution(18156060135148101076)
XLA Ops:
  0.0 0.7 %constant_dynamic-update-slice_fusion.1 = bf16[8,1280]{1,0:T(8,128)(2,1)S(1)} fusion(bf16[8,768]{1,0:T(8,128)(2,1)} %param.6), kind=kLoop, calls=%fused_computation.4 | loop fusion | bytes 24576
  0.7 0.7 %constant_dynamic-update-slice_fusion = bf16[8,1280]{1,0:T(8,128)(2,1)S(1)} fusion(bf16[8,1280]{1,0:T(8,128)(2,1)S(1)} %constant_dynamic-update-slice_fusion.1, bf16[8,512]{1,0:T(8,128)(2,1)} %param.7), kind=kLoop, calls=%fused_computation.3 | loop fusion | bytes 16384 | tf_op jit(solution)/shard_map/concatenate | solution.py:123
  1.4 3.5 %collective-permute-start = (bf16[8,1280]{1,0:T(8,128)(2,1)S(1)}, bf16[8,1280]{1,0:T(8,128)(2,1)S(1)}, u32[]{:S(2)}, u32[]{:S(2)}) collective-permute-start(bf16[8,1280]{1,0:T(8,128)(2,1)S(1)} %constant_dynamic-update-slice_fusion), channel_id=1, source_target_pairs={{0,9},{1,8},{2,11},{3,10},{4,13},{5,12},{6,15},{7,14},{8,1},{9,0},... | collective-permute-start | bytes 61448 | tf_op jit(solution)/shard_map/ppermute | solution.py:33
  4.9 1.5 %collective-permute-done = bf16[8,1280]{1,0:T(8,128)(2,1)S(1)} collective-permute-done((bf16[8,1280]{1,0:T(8,128)(2,1)S(1)}, bf16[8,1280]{1,0:T(8,128)(2,1)S(1)}, u32[]{:S(2)}, u32[]{:S(2)}) %collective-permute-start) | collective-permute-done | bytes 20512 | tf_op jit(solution)/shard_map/ppermute | solution.py:33
  6.4 1.9 %collective-permute-start.1 = (bf16[16,1280]{1,0:T(8,128)(2,1)S(1)}, bf16[16,1280]{1,0:T(8,128)(2,1)S(1)}, u32[]{:S(2)}, u32[]{:S(2)}) collective-permute-start(bf16[16,1280]{1,0:T(8,128)(2,1)S(1)} %pad_maximum_fusion.2), channel_id=1, source_target_pairs={{0,5},{1,4},{2,7},{3,6},{4,1},{5,0},{6,3},{7,2},{8,13},{9,12},{10,... | collective-permute-start | bytes 122888 | tf_op jit(solution)/shard_map/ppermute | solution.py:33
  8.3 1.7 %collective-permute-done.1 = bf16[16,1280]{1,0:T(8,128)(2,1)S(1)} collective-permute-done((bf16[16,1280]{1,0:T(8,128)(2,1)S(1)}, bf16[16,1280]{1,0:T(8,128)(2,1)S(1)}, u32[]{:S(2)}, u32[]{:S(2)}) %collective-permute-start.1) | collective-permute-done | bytes 40992 | tf_op jit(solution)/shard_map/ppermute | solution.py:33
  10.0 1.8 %collective-permute-start.2 = (bf16[32,1280]{1,0:T(8,128)(2,1)S(1)}, bf16[32,1280]{1,0:T(8,128)(2,1)S(1)}, u32[]{:S(2)}, u32[]{:S(2)}) collective-permute-start(bf16[32,1280]{1,0:T(8,128)(2,1)S(1)} %pad_maximum_fusion.1), channel_id=1, source_target_pairs={{0,3},{1,2},{2,1},{3,0},{4,7},{5,6},{6,5},{7,4},{8,11},{9,10},{10,... | collective-permute-start | bytes 245768 | tf_op jit(solution)/shard_map/ppermute | solution.py:33
  11.8 2.5 %collective-permute-done.2 = bf16[32,1280]{1,0:T(8,128)(2,1)S(1)} collective-permute-done((bf16[32,1280]{1,0:T(8,128)(2,1)S(1)}, bf16[32,1280]{1,0:T(8,128)(2,1)S(1)}, u32[]{:S(2)}, u32[]{:S(2)}) %collective-permute-start.2) | collective-permute-done | bytes 81952 | tf_op jit(solution)/shard_map/ppermute | solution.py:33
  14.3 0.3 %collective-permute-start.3 = (bf16[64,1280]{1,0:T(8,128)(2,1)S(1)}, bf16[64,1280]{1,0:T(8,128)(2,1)S(1)}, u32[]{:S(2)}, u32[]{:S(2)}) collective-permute-start(bf16[64,1280]{1,0:T(8,128)(2,1)S(1)} %pad_maximum_fusion.refs_1_), channel_id=1, source_target_pairs={{0,1},{1,0},{2,3},{3,2},{4,5},{5,4},{6,7},{7,6},{8,9},{9,8},{10,11... | collective-permute-start | bytes 491528 | tf_op jit(solution)/shard_map/ppermute | solution.py:35
  15.3 0.5 %collective-permute-done.3.refs_2_ = bf16[64,1280]{1,0:T(8,128)(2,1)S(1)} collective-permute-done((bf16[64,1280]{1,0:T(8,128)(2,1)S(1)}, bf16[64,1280]{1,0:T(8,128)(2,1)S(1)}, u32[]{:S(2)}, u32[]{:S(2)}) %collective-permute-start.3) | collective-permute-done | bytes 163872 | tf_op jit(solution)/shard_map/ppermute | solution.py:35
  15.8 0.0 copy-start
  15.8 1.9 %copy-done = bf16[128,12288]{1,0:T(8,128)(2,1)S(1)} copy-done((bf16[128,12288]{1,0:T(8,128)(2,1)S(1)}, bf16[128,12288]{1,0:T(8,128)(2,1)}, u32[]{:S(2)}) %copy-start) | copy-done | bytes 3145752
  17.7 0.0 copy-start.1
  17.7 0.7 %copy-done.1 = s32[32]{0:T(128)S(1)} copy-done((s32[32]{0:T(128)S(1)}, s32[32]{0:T(128)}, u32[]{:S(2)}) %copy-start.1) | copy-done | bytes 152
  18.4 4.7 %shard_map.55 = bf16[128,8192]{1,0:T(8,128)(2,1)} custom-call(bf16[128,12288]{1,0:T(8,128)(2,1)S(1)} %copy-done, bf16[64,1280]{1,0:T(8,128)(2,1)S(1)} %pad_maximum_fusion.refs_1_, bf16[64,1280]{1,0:T(8,128)(2,1)S(1)} %collective-permute-done.3.refs_2_, s32[32]{0:T(128)S(1)} %copy-done.1, s32[1]{0:T(128)S(6)} %copy.7.refs_4_), custom_call_target="tpu_custom_call" | custom-call | tf_op jit(solution)/shard_map/pallas_call | solution.py:126
  (3 shorter events, 0.0 us)
Async XLA Ops:
  1.4 5.0 %collective-permute-start = (bf16[8,1280]{1,0:T(8,128)(2,1)S(1)}, bf16[8,1280]{1,0:T(8,128)(2,1)S(1)}, u32[]{:S(2)}, u32[]{:S(2)}) collective-permute-start(bf16[8,1280]{1,0:T(8,128)(2,1)S(1)} %constant_dynamic-update-slice_fusion), channel_id=1, source_target_pairs={{0,9},{1,8},{2,11},{3,10},{4,13},{5,12},{6,15},{7,14},{8,1},{9,0},... | collective-permute-start | bytes 61448 | tf_op jit(solution)/shard_map/ppermute | solution.py:33
  6.4 3.5 %collective-permute-start.1 = (bf16[16,1280]{1,0:T(8,128)(2,1)S(1)}, bf16[16,1280]{1,0:T(8,128)(2,1)S(1)}, u32[]{:S(2)}, u32[]{:S(2)}) collective-permute-start(bf16[16,1280]{1,0:T(8,128)(2,1)S(1)} %pad_maximum_fusion.2), channel_id=1, source_target_pairs={{0,5},{1,4},{2,7},{3,6},{4,1},{5,0},{6,3},{7,2},{8,13},{9,12},{10,... | collective-permute-start | bytes 122888 | tf_op jit(solution)/shard_map/ppermute | solution.py:33
  10.0 4.3 %collective-permute-start.2 = (bf16[32,1280]{1,0:T(8,128)(2,1)S(1)}, bf16[32,1280]{1,0:T(8,128)(2,1)S(1)}, u32[]{:S(2)}, u32[]{:S(2)}) collective-permute-start(bf16[32,1280]{1,0:T(8,128)(2,1)S(1)} %pad_maximum_fusion.1), channel_id=1, source_target_pairs={{0,3},{1,2},{2,1},{3,0},{4,7},{5,6},{6,5},{7,4},{8,11},{9,10},{10,... | collective-permute-start | bytes 245768 | tf_op jit(solution)/shard_map/ppermute | solution.py:33
  14.3 1.5 %collective-permute-start.3 = (bf16[64,1280]{1,0:T(8,128)(2,1)S(1)}, bf16[64,1280]{1,0:T(8,128)(2,1)S(1)}, u32[]{:S(2)}, u32[]{:S(2)}) collective-permute-start(bf16[64,1280]{1,0:T(8,128)(2,1)S(1)} %pad_maximum_fusion.refs_1_), channel_id=1, source_target_pairs={{0,1},{1,0},{2,3},{3,2},{4,5},{5,4},{6,7},{7,6},{8,9},{9,8},{10,11... | collective-permute-start | bytes 491528 | tf_op jit(solution)/shard_map/ppermute | solution.py:35
  15.8 1.9 %copy-start = (bf16[128,12288]{1,0:T(8,128)(2,1)S(1)}, bf16[128,12288]{1,0:T(8,128)(2,1)}, u32[]{:S(2)}) copy-start(bf16[128,12288]{1,0:T(8,128)(2,1)} %refs_0_.1) | copy-start | bytes 9437188
  17.7 0.7 %copy-start.1 = (s32[32]{0:T(128)S(1)}, s32[32]{0:T(128)}, u32[]{:S(2)}) copy-start(s32[32]{0:T(128)} %refs_3_.1) | copy-start | bytes 388

commit v2 on v1

--- a/solution.py
+++ b/solution.py
@@ -8,6 +8,7 @@
 from jax.experimental.pallas import tpu as pltpu
 from jax.sharding import PartitionSpec as P
 
+
 H = 64
 G = 4
 DK = 192
@@ -17,6 +18,7 @@
 QB = 64
 PER = H // G
 HIDDEN = -1e30
+STAGE_BYTES = 1024 * 1024
 
 
 def exchange_masks(count):
@@ -29,19 +31,15 @@
         whole = lax.all_gather(x, "seq", axis=0, tiled=True)
         return [whole], None
     masks = exchange_masks(count)
-    for mask in masks[:-1]:
+    for bit, mask in enumerate(masks):
         other = lax.ppermute(x, "seq", [(i, i ^ mask) for i in range(count)])
-        x = jnp.concatenate([x, other], axis=0)
-    other = lax.ppermute(x, "seq", [(i, i ^ masks[-1]) for i in range(count)])
+        if bit < len(masks) - 1:
+            x = jnp.concatenate([x, other], axis=0)
     return [x, other], masks
 
 
-def attend(masks, shard, parts, *refs):
-    q_ref, *kv_refs = refs[: 1 + parts]
-    limits_ref, valid_ref, out_ref, o_ref, sem = refs[1 + parts :]
-    tokens = q_ref.shape[0]
-    total = sum(r.shape[0] for r in kv_refs)
-    blocks = tokens // QB
+def stage(masks, shard, limits_ref, valid_ref, bias_ref):
+    blocks, total = bias_ref.shape[0] // 8, bias_ref.shape[1]
     me = lax.axis_index("seq")
     usable = jnp.maximum(((valid_ref[0] - CBLOCK) >> (STRIDE.bit_length() - 1)) + 1, 1)
     lane = lax.broadcasted_iota(jnp.int32, (8, total), 1)
@@ -53,10 +51,18 @@
         for bit, mask in enumerate(masks):
             owner = owner ^ (((lane >> (low + bit)) & 1) * mask)
         ids = owner * shard + (lane & (shard - 1))
-    biases = [
-        jnp.where(ids < jnp.minimum(limits_ref[me * blocks + b], usable), 0.0, HIDDEN)[:1]
-        for b in range(blocks)
-    ]
+    for b in range(blocks):
+        cap = jnp.minimum(limits_ref[me * blocks + b], usable)
+        bias_ref[8 * b : 8 * b + 8] = jnp.where(ids < cap, 0.0, HIDDEN)
+
+
+def attend(parts, *refs):
+    q_ref, bias_ref, *kv_refs = refs[: 2 + parts]
+    out_ref, o_ref, sem = refs[2 + parts :]
+    tokens = q_ref.shape[0]
+    total = sum(r.shape[0] for r in kv_refs)
+    blocks = tokens // QB
+    biases = [bias_ref[8 * b : 8 * b + 1] for b in range(blocks)]
     factor = math.log2(math.e) * float(DK) ** -0.5
     wide = 2 * DV
     col = lax.broadcasted_iota(jnp.int32, (total, wide), 1)
@@ -117,20 +123,40 @@
         copy.wait()
 
 
-def per_device(count, queries, sum_keys, sum_values, limits, valid_tokens):
+def layer(count, queries, sum_keys, sum_values, limits, valid_tokens):
     tokens = queries.shape[0]
     shard = sum_keys.shape[0]
-    halves, masks = gather_parts(jnp.concatenate([sum_keys, sum_values], axis=1), count)
     vmem = pl.BlockSpec(memory_space=pltpu.VMEM)
     smem = pl.BlockSpec(memory_space=pltpu.SMEM)
+    hbm = pl.BlockSpec(memory_space=pl.ANY)
+    low = jnp.array(-jnp.inf, sum_keys.dtype)
+    packed = jnp.maximum(
+        lax.pad(sum_keys, low, ((0, 0, 0), (0, sum_values.shape[1], 0))),
+        lax.pad(sum_values, low, ((0, 0, 0), (sum_keys.shape[1], 0, 0))),
+    )
+    halves, masks = gather_parts(packed, count)
+    biases = pl.pallas_call(
+        functools.partial(stage, masks, shard),
+        out_shape=jax.ShapeDtypeStruct((tokens // QB * 8, shard * count), jnp.float32),
+        in_specs=[smem, smem],
+        out_specs=vmem,
+        cost_estimate=pl.CostEstimate(flops=40_000_000_000, bytes_accessed=80_000_000, transcendentals=0),
+        compiler_params=pltpu.CompilerParams(vmem_limit_bytes=STAGE_BYTES),
+        name="stage",
+    )(limits, valid_tokens)
     return pl.pallas_call(
-        functools.partial(attend, masks, shard, len(halves)),
+        functools.partial(attend, len(halves)),
         out_shape=jax.ShapeDtypeStruct((tokens, H * DV), jnp.bfloat16),
-        in_specs=[vmem] * (1 + len(halves)) + [smem, smem],
-        out_specs=pl.BlockSpec(memory_space=pl.ANY),
+        in_specs=[vmem] * (2 + len(halves)),
+        out_specs=hbm,
         scratch_shapes=[pltpu.VMEM((tokens, H * DV), jnp.bfloat16), pltpu.SemaphoreType.DMA((G,))],
         compiler_params=pltpu.CompilerParams(vmem_limit_bytes=40 * 1024 * 1024),
-    )(queries, *halves, limits, valid_tokens)
+        name="attend",
+    )(queries, biases, *halves)
+
+
+def per_device(count, *args):
+    return layer(count, *args)
 
 
 def solution(mesh):

time: 23.4 us -> 20.1 us (0.86)
  local copies, waits for them, and re-layouts: 3.95 us -> 0.98 us
  waiting for transfers between devices: 6.21 us -> 5.09 us
  other arithmetic: 0.02 us -> 0.75 us
    unnamed x5 -> x4, local copies, waits for them, and re-layouts: 3.25 us -> 0.98 us
    max x0 -> x1, other arithmetic: none -> 0.73 us  [layer(): jnp.maximum(lax.pad(sum_keys, low, ((0, 0, 0), (0, sum_values.shape[1], 0...]
    concatenate x1 -> x0, local copies, waits for them, and re-layouts: 0.7 us -> none  [per_device(): jnp.concatenate([sum_keys, sum_values], axis=1)]
    ppermute x3 -> x4, waiting for transfers between devices: 5.74 us -> 5.09 us  [gather_parts(): other = lax.ppermute(x, 'seq', [(i, i ^ mask) for i in range(count)])]
    ppermute x1 -> x0, waiting for transfers between devices: 0.46 us -> none  [gather_parts(): other = lax.ppermute(x, 'seq', [(i, i ^ masks[-1]) for i in range(count)])]
    ppermute x1 -> x0, starting transfers between devices: 0.35 us -> none  [gather_parts(): other = lax.ppermute(x, 'seq', [(i, i ^ masks[-1]) for i in range(count)])]
    ppermute x3 -> x4, starting transfers between devices: 7.16 us -> 7.51 us  [gather_parts(): other = lax.ppermute(x, 'seq', [(i, i ^ mask) for i in range(count)])]
    pallas_call x1 -> x2, Pallas kernels: 4.66 us -> 4.7 us  [the longest x1 4.15 us: layer(): pl.pallas_call(functools.partial(attend, len(halves)), out_shape=jax.Shap...]
  transfers between devices with their start and end apart: 4 -> 4, of which waited for: 4 -> 3; matrix products, arithmetic and copies ran while one was open for 0% -> 0% of each run, Pallas kernels for 0% -> 3%
where the time goes in v2:
time: 20.1 us; the launch traced here: 19.7 us
  starting transfers between devices  7.51 us (37%)
  waiting for transfers between devices  5.09 us (25%)
  Pallas kernels  4.7 us (23%)
  local copies, waits for them, and re-layouts  0.98 us (5%)
  other arithmetic  0.75 us (4%)
  between operations  0.69 us (3%)
    ppermute x4, starting transfers between devices, gather_parts(): other = lax.ppermute(x, 'seq', [(i, i ^ mask) for i in range(count)])  7.51 us
    ppermute x4, waiting for transfers between devices, gather_parts(): other = lax.ppermute(x, 'seq', [(i, i ^ mask) for i in range(count)])  5.09 us
    pallas_call x1, Pallas kernels, layer(): pl.pallas_call(functools.partial(attend, len(halves)), out_shape=jax.Shap...  4.15 us
    unnamed x4, local copies, waits for them, and re-layouts  0.98 us
    max x1, other arithmetic, layer(): jnp.maximum(lax.pad(sum_keys, low, ((0, 0, 0), (0, sum_values.shape[1], 0...  0.73 us
    pallas_call x1, Pallas kernels, layer(): pl.pallas_call(functools.partial(stage, masks, shard), out_shape=jax.Shap...  0.55 us
  transfers between devices with their start and end apart: 4, of which 3 were waited for; matrix products, arithmetic and copies ran while one was open for 0% of the time, Pallas kernels for 3%

profile of v2, /device:TPU:0, one launch (start us, length us, event | category | flops | bytes accessed | tf_op | source)
XLA Modules:
  0.0 19.7 jit_solution(1762423788050370791)
XLA Ops:
  0.0 0.7 %pad_maximum_fusion.3 = bf16[8,1280]{1,0:T(8,128)(2,1)S(1)} fusion(bf16[8,512]{1,0:T(8,128)(2,1)} %param.7, bf16[8,768]{1,0:T(8,128)(2,1)} %param.6), kind=kLoop, calls=%fused_computation.3 | loop fusion | flops 40960 | bytes 40960 | tf_op jit(solution)/shard_map/max | solution.py:133
  0.7 3.5 %collective-permute-start = (bf16[8,1280]{1,0:T(8,128)(2,1)S(1)}, bf16[8,1280]{1,0:T(8,128)(2,1)S(1)}, u32[]{:S(2)}, u32[]{:S(2)}) collective-permute-start(bf16[8,1280]{1,0:T(8,128)(2,1)S(1)} %pad_maximum_fusion.3), channel_id=1, source_target_pairs={{0,9},{1,8},{2,11},{3,10},{4,13},{5,12},{6,15},{7,14},{8,1},{9,0},... | collective-permute-start | bytes 61448 | tf_op jit(solution)/shard_map/ppermute | solution.py:35
  4.2 1.5 %collective-permute-done = bf16[8,1280]{1,0:T(8,128)(2,1)S(1)} collective-permute-done((bf16[8,1280]{1,0:T(8,128)(2,1)S(1)}, bf16[8,1280]{1,0:T(8,128)(2,1)S(1)}, u32[]{:S(2)}, u32[]{:S(2)}) %collective-permute-start) | collective-permute-done | bytes 20512 | tf_op jit(solution)/shard_map/ppermute | solution.py:35
  5.8 1.9 %collective-permute-start.1 = (bf16[16,1280]{1,0:T(8,128)(2,1)S(1)}, bf16[16,1280]{1,0:T(8,128)(2,1)S(1)}, u32[]{:S(2)}, u32[]{:S(2)}) collective-permute-start(bf16[16,1280]{1,0:T(8,128)(2,1)S(1)} %pad_maximum_fusion.2), channel_id=1, source_target_pairs={{0,5},{1,4},{2,7},{3,6},{4,1},{5,0},{6,3},{7,2},{8,13},{9,12},{10,... | collective-permute-start | bytes 122888 | tf_op jit(solution)/shard_map/ppermute | solution.py:35
  7.6 1.7 %collective-permute-done.1 = bf16[16,1280]{1,0:T(8,128)(2,1)S(1)} collective-permute-done((bf16[16,1280]{1,0:T(8,128)(2,1)S(1)}, bf16[16,1280]{1,0:T(8,128)(2,1)S(1)}, u32[]{:S(2)}, u32[]{:S(2)}) %collective-permute-start.1) | collective-permute-done | bytes 40992 | tf_op jit(solution)/shard_map/ppermute | solution.py:35
  9.3 1.8 %collective-permute-start.2 = (bf16[32,1280]{1,0:T(8,128)(2,1)S(1)}, bf16[32,1280]{1,0:T(8,128)(2,1)S(1)}, u32[]{:S(2)}, u32[]{:S(2)}) collective-permute-start(bf16[32,1280]{1,0:T(8,128)(2,1)S(1)} %pad_maximum_fusion.1), channel_id=1, source_target_pairs={{0,3},{1,2},{2,1},{3,0},{4,7},{5,6},{6,5},{7,4},{8,11},{9,10},{10,... | collective-permute-start | bytes 245768 | tf_op jit(solution)/shard_map/ppermute | solution.py:35
  11.8 1.9 %collective-permute-done.2 = bf16[32,1280]{1,0:T(8,128)(2,1)S(1)} collective-permute-done((bf16[32,1280]{1,0:T(8,128)(2,1)S(1)}, bf16[32,1280]{1,0:T(8,128)(2,1)S(1)}, u32[]{:S(2)}, u32[]{:S(2)}) %collective-permute-start.2) | collective-permute-done | bytes 81952 | tf_op jit(solution)/shard_map/ppermute | solution.py:35
  13.7 0.0 copy-start
  13.7 0.3 %collective-permute-start.3 = (bf16[64,1280]{1,0:T(8,128)(2,1)S(1)}, bf16[64,1280]{1,0:T(8,128)(2,1)S(1)}, u32[]{:S(2)}, u32[]{:S(2)}) collective-permute-start(bf16[64,1280]{1,0:T(8,128)(2,1)S(1)} %pad_maximum_fusion.refs_2_), channel_id=1, source_target_pairs={{0,1},{1,0},{2,3},{3,2},{4,5},{5,4},{6,7},{7,6},{8,9},{9,8},{10,11... | collective-permute-start | bytes 491528 | tf_op jit(solution)/shard_map/ppermute | solution.py:35
  14.0 0.0 copy-start.1
  14.0 0.8 %copy-done.1 = s32[32]{0:T(128)S(1)} copy-done((s32[32]{0:T(128)S(1)}, s32[32]{0:T(128)}, u32[]{:S(2)}) %copy-start.1) | copy-done | bytes 152
  14.9 0.6 %stage.1.refs_1_ = f32[16,128]{1,0:T(8,128)S(1)} custom-call(s32[32]{0:T(128)S(1)} %copy-done.1, s32[1]{0:T(128)S(6)} %copy.6.valid_ref), custom_call_target="tpu_custom_call" | custom-call | flops 40000000000 | bytes 80000000 | tf_op jit(solution)/shard_map/stage/pallas_call | solution.py:138
  15.4 0.0 collective-permute-done.3.refs_3_
  15.4 0.1 copy-done
  15.6 4.1 %attend.1 = bf16[128,8192]{1,0:T(8,128)(2,1)} custom-call(bf16[128,12288]{1,0:T(8,128)(2,1)S(1)} %copy-done, f32[16,128]{1,0:T(8,128)S(1)} %stage.1.refs_1_, bf16[64,1280]{1,0:T(8,128)(2,1)S(1)} %pad_maximum_fusion.refs_2_, bf16[64,1280]{1,0:T(8,128)(2,1)S(1)} %collective-permute-done.3.refs_3_), custom_call_target="tpu_custom_call" | custom-call | tf_op jit(solution)/shard_map/attend/pallas_call | solution.py:147
  (3 shorter events, 0.0 us)
Async XLA Ops:
  0.7 5.0 %collective-permute-start = (bf16[8,1280]{1,0:T(8,128)(2,1)S(1)}, bf16[8,1280]{1,0:T(8,128)(2,1)S(1)}, u32[]{:S(2)}, u32[]{:S(2)}) collective-permute-start(bf16[8,1280]{1,0:T(8,128)(2,1)S(1)} %pad_maximum_fusion.3), channel_id=1, source_target_pairs={{0,9},{1,8},{2,11},{3,10},{4,13},{5,12},{6,15},{7,14},{8,1},{9,0},... | collective-permute-start | bytes 61448 | tf_op jit(solution)/shard_map/ppermute | solution.py:35
  5.8 3.5 %collective-permute-start.1 = (bf16[16,1280]{1,0:T(8,128)(2,1)S(1)}, bf16[16,1280]{1,0:T(8,128)(2,1)S(1)}, u32[]{:S(2)}, u32[]{:S(2)}) collective-permute-start(bf16[16,1280]{1,0:T(8,128)(2,1)S(1)} %pad_maximum_fusion.2), channel_id=1, source_target_pairs={{0,5},{1,4},{2,7},{3,6},{4,1},{5,0},{6,3},{7,2},{8,13},{9,12},{10,... | collective-permute-start | bytes 122888 | tf_op jit(solution)/shard_map/ppermute | solution.py:35
  9.3 4.3 %collective-permute-start.2 = (bf16[32,1280]{1,0:T(8,128)(2,1)S(1)}, bf16[32,1280]{1,0:T(8,128)(2,1)S(1)}, u32[]{:S(2)}, u32[]{:S(2)}) collective-permute-start(bf16[32,1280]{1,0:T(8,128)(2,1)S(1)} %pad_maximum_fusion.1), channel_id=1, source_target_pairs={{0,3},{1,2},{2,1},{3,0},{4,7},{5,6},{6,5},{7,4},{8,11},{9,10},{10,... | collective-permute-start | bytes 245768 | tf_op jit(solution)/shard_map/ppermute | solution.py:35
  13.7 1.9 %copy-start = (bf16[128,12288]{1,0:T(8,128)(2,1)S(1)}, bf16[128,12288]{1,0:T(8,128)(2,1)}, u32[]{:S(2)}) copy-start(bf16[128,12288]{1,0:T(8,128)(2,1)} %refs_0_.1) | copy-start | bytes 9437188
  13.7 1.7 %collective-permute-start.3 = (bf16[64,1280]{1,0:T(8,128)(2,1)S(1)}, bf16[64,1280]{1,0:T(8,128)(2,1)S(1)}, u32[]{:S(2)}, u32[]{:S(2)}) collective-permute-start(bf16[64,1280]{1,0:T(8,128)(2,1)S(1)} %pad_maximum_fusion.refs_2_), channel_id=1, source_target_pairs={{0,1},{1,0},{2,3},{3,2},{4,5},{5,4},{6,7},{7,6},{8,9},{9,8},{10,11... | collective-permute-start | bytes 491528 | tf_op jit(solution)/shard_map/ppermute | solution.py:35
  14.0 0.8 %copy-start.1 = (s32[32]{0:T(128)S(1)}, s32[32]{0:T(128)}, u32[]{:S(2)}) copy-start(s32[32]{0:T(128)} %limits_ref.1) | copy-start | bytes 388

commit v3 on v2

--- a/solution.py
+++ b/solution.py
@@ -18,6 +18,8 @@
 QB = 64
 PER = H // G
 HIDDEN = -1e30
+CHUNK = 4
+LAG = 2
 STAGE_BYTES = 1024 * 1024
 
 
@@ -77,50 +79,89 @@
         return jnp.where((col >= offset) & (col < offset + DK), window, 0.0).astype(jnp.bfloat16)
 
     pairs = PER // 2
-    copies = []
-    for g in range(G):
-        v_start = G * DK + g * DV
-        values = jnp.concatenate([r[:, v_start : v_start + DV] for r in kv_refs], axis=0)
-        sides = []
+    chunk = min(CHUNK, pairs)
+    units = [(g, c) for g in range(G) for c in range(0, pairs, chunk)]
+    keys, mixes = {}, {}
+
+    def score(g, c):
+        if g not in keys:
+            keys[g] = [keys_at(g, side * (wide - DK)) for side in range(2)]
+        both = []
         for side in range(2):
-            weights = keys_at(g, side * (wide - DK))
             q0 = g * PER * DK + side * 128
             rows = jnp.concatenate(
-                [q_ref[:, q0 + j * 2 * DK : q0 + j * 2 * DK + wide] for j in range(pairs)], axis=0
+                [q_ref[:, q0 + j * 2 * DK : q0 + j * 2 * DK + wide] for j in range(c, c + chunk)], axis=0
             )
-            scores = lax.dot_general(
-                rows, weights, (((1,), (1,)), ((), ())), preferred_element_type=jnp.float32
+            both.append(
+                lax.dot_general(
+                    rows, keys[g][side], (((1,), (1,)), ((), ())), preferred_element_type=jnp.float32
+                )
             )
-            scores = scores.reshape(pairs, blocks, QB, total)
-            scores = jnp.concatenate([scores[:, b : b + 1] + biases[b] for b in range(blocks)], axis=1)
-            scores = scores.reshape(pairs * tokens, total)
-            top = jnp.max(scores, axis=1, keepdims=True)
-            w = jnp.exp2((scores - top) * factor)
-            norm = jnp.sum(w, axis=1, keepdims=True)
-            sides.append((w.astype(jnp.bfloat16), 1.0 / norm))
-        (wa, ra), (wb, rb) = sides
-        if total <= 128:
-            zeros = jnp.zeros_like(values)
-            both = jnp.concatenate(
-                [jnp.concatenate([values, zeros], axis=1), jnp.concatenate([zeros, values], axis=1)], axis=0
-            )
-            out = jnp.dot(jnp.concatenate([wa, wb], axis=1), both, preferred_element_type=jnp.float32)
-            outa, outb = out[:, :DV], out[:, DV:]
-        else:
-            outa = jnp.dot(wa, values, preferred_element_type=jnp.float32)
-            outb = jnp.dot(wb, values, preferred_element_type=jnp.float32)
-        outa = (outa * ra).astype(jnp.bfloat16)
-        outb = (outb * rb).astype(jnp.bfloat16)
-        for j in range(pairs):
-            at = (g * PER + 2 * j) * DV
-            o_ref[:, at : at + DV] = outa[j * tokens : (j + 1) * tokens]
-            o_ref[:, at + DV : at + 2 * DV] = outb[j * tokens : (j + 1) * tokens]
-        span = pl.ds(g * PER * DV, PER * DV)
-        copy = pltpu.make_async_copy(o_ref.at[:, span], out_ref.at[:, span], sem.at[g])
-        copy.start()
-        copies.append(copy)
+        return both
+
+    def soften(side, scores):
+        scores = scores.reshape(chunk, blocks, QB, total)
+        scores = jnp.concatenate([scores[:, b : b + 1] + biases[b] for b in range(blocks)], axis=1)
+        scores = scores.reshape(chunk * tokens, total)
+        top = jnp.max(scores, axis=1, keepdims=True)
+        w = jnp.exp2((scores - top) * factor)
+        p = w.astype(jnp.bfloat16)
+        if side:
+            return p, jnp.sum(w, axis=1, keepdims=True)
+        rest = (w - p.astype(jnp.float32)).astype(jnp.bfloat16)
+        return jnp.concatenate([p, rest], axis=1), None
+
+    def mix(g, side):
+        if (g, side) not in mixes:
+            v_start = G * DK + g * DV
+            values = jnp.concatenate([r[:, v_start : v_start + DV] for r in kv_refs], axis=0)
+            if not side:
+                ones, zeros = jnp.ones_like(values), jnp.zeros_like(values)
+                values = jnp.concatenate(
+                    [jnp.concatenate([values, ones], axis=1), jnp.concatenate([zeros, ones], axis=1)], axis=0
+                )
+            mixes[g, side] = values
+        return mixes[g, side]
+
+    def place(g, c, out, scale, side):
+        out = (out * scale).astype(jnp.bfloat16)
+        for j in range(chunk):
+            at = (g * PER + 2 * (c + j) + side) * DV
+            o_ref[:, at : at + DV] = out[j * tokens : (j + 1) * tokens]
+
+    copies = []
+    scored = {}
+    for u in range(len(units) + LAG):
+        if u < len(units):
+            scored[u] = score(*units[u])
+        p = u - LAG
+        if p >= 0:
+            g, c = units[p]
+            for side, (w, norm) in enumerate([soften(i, x) for i, x in enumerate(scored.pop(p))]):
+                out = jnp.dot(w, mix(g, side), preferred_element_type=jnp.float32)
+                if norm is None:
+                    norm = out[:, DV:]
+                place(g, c, out[:, :DV], 1.0 / norm, side)
+            span = pl.ds((g * PER + 2 * c) * DV, 2 * chunk * DV)
+            copy = pltpu.make_async_copy(o_ref.at[:, span], out_ref.at[:, span], sem.at[p])
+            copy.start()
+            copies.append(copy)
     for copy in copies:
         copy.wait()
+
+
+def attend_call(queries, biases, halves):
+    tokens = queries.shape[0]
+    vmem = pl.BlockSpec(memory_space=pltpu.VMEM)
+    return pl.pallas_call(
+        functools.partial(attend, len(halves)),
+        out_shape=jax.ShapeDtypeStruct((tokens, H * DV), jnp.bfloat16),
+        in_specs=[vmem] * (2 + len(halves)),
+        out_specs=pl.BlockSpec(memory_space=pl.ANY),
+        scratch_shapes=[pltpu.VMEM((tokens, H * DV), jnp.bfloat16), pltpu.SemaphoreType.DMA((H // (2 * CHUNK),))],
+        compiler_params=pltpu.CompilerParams(vmem_limit_bytes=40 * 1024 * 1024),
+        name="attend",
+    )(queries, biases, *halves)
 
 
 def layer(count, queries, sum_keys, sum_values, limits, valid_tokens):
@@ -128,7 +169,6 @@
     shard = sum_keys.shape[0]
     vmem = pl.BlockSpec(memory_space=pltpu.VMEM)
     smem = pl.BlockSpec(memory_space=pltpu.SMEM)
-    hbm = pl.BlockSpec(memory_space=pl.ANY)
     low = jnp.array(-jnp.inf, sum_keys.dtype)
     packed = jnp.maximum(
         lax.pad(sum_keys, low, ((0, 0, 0), (0, sum_values.shape[1], 0))),
@@ -144,15 +184,7 @@
         compiler_params=pltpu.CompilerParams(vmem_limit_bytes=STAGE_BYTES),
         name="stage",
     )(limits, valid_tokens)
-    return pl.pallas_call(
-        functools.partial(attend, len(halves)),
-        out_shape=jax.ShapeDtypeStruct((tokens, H * DV), jnp.bfloat16),
-        in_specs=[vmem] * (2 + len(halves)),
-        out_specs=hbm,
-        scratch_shapes=[pltpu.VMEM((tokens, H * DV), jnp.bfloat16), pltpu.SemaphoreType.DMA((G,))],
-        compiler_params=pltpu.CompilerParams(vmem_limit_bytes=40 * 1024 * 1024),
-        name="attend",
-    )(queries, biases, *halves)
+    return attend_call(queries, biases, halves)
 
 
 def per_device(count, *args):

time: 20.1 us -> 19.2 us (0.955)
  Pallas kernels: 4.7 us -> 3.78 us
    pallas_call x1, Pallas kernels: 4.15 us -> 3.23 us  [attend_call(): pl.pallas_call(functools.partial(attend, len(halves)), out_shape=jax.Shap...]
where the time goes in v3:
time: 19.2 us; the launch traced here: 18.8 us
  starting transfers between devices  7.51 us (39%)
  waiting for transfers between devices  5.09 us (27%)
  Pallas kernels  3.78 us (20%)
  local copies, waits for them, and re-layouts  0.98 us (5%)
  other arithmetic  0.75 us (4%)
  between operations  0.69 us (4%)
    ppermute x4, starting transfers between devices, gather_parts(): other = lax.ppermute(x, 'seq', [(i, i ^ mask) for i in range(count)])  7.51 us
    ppermute x4, waiting for transfers between devices, gather_parts(): other = lax.ppermute(x, 'seq', [(i, i ^ mask) for i in range(count)])  5.09 us
    pallas_call x1, Pallas kernels, attend_call(): pl.pallas_call(functools.partial(attend, len(halves)), out_shape=jax.Shap...  3.23 us
    unnamed x4, local copies, waits for them, and re-layouts  0.98 us
    max x1, other arithmetic, layer(): jnp.maximum(lax.pad(sum_keys, low, ((0, 0, 0), (0, sum_values.shape[1], 0...  0.73 us
    pallas_call x1, Pallas kernels, layer(): pl.pallas_call(functools.partial(stage, masks, shard), out_shape=jax.Shap...  0.55 us
  transfers between devices with their start and end apart: 4, of which 3 were waited for; matrix products, arithmetic and copies ran while one was open for 0% of the time, Pallas kernels for 3%

profile of v3, /device:TPU:0, one launch (start us, length us, event | category | flops | bytes accessed | tf_op | source)
XLA Modules:
  0.0 18.8 jit_solution(1818991179056185299)
XLA Ops:
  0.0 0.7 %pad_maximum_fusion.3 = bf16[8,1280]{1,0:T(8,128)(2,1)S(1)} fusion(bf16[8,512]{1,0:T(8,128)(2,1)} %param.7, bf16[8,768]{1,0:T(8,128)(2,1)} %param.6), kind=kLoop, calls=%fused_computation.3 | loop fusion | flops 40960 | bytes 40960 | tf_op jit(solution)/shard_map/max | solution.py:173
  0.7 3.5 %collective-permute-start = (bf16[8,1280]{1,0:T(8,128)(2,1)S(1)}, bf16[8,1280]{1,0:T(8,128)(2,1)S(1)}, u32[]{:S(2)}, u32[]{:S(2)}) collective-permute-start(bf16[8,1280]{1,0:T(8,128)(2,1)S(1)} %pad_maximum_fusion.3), channel_id=1, source_target_pairs={{0,9},{1,8},{2,11},{3,10},{4,13},{5,12},{6,15},{7,14},{8,1},{9,0},... | collective-permute-start | bytes 61448 | tf_op jit(solution)/shard_map/ppermute | solution.py:37
  4.2 1.5 %collective-permute-done = bf16[8,1280]{1,0:T(8,128)(2,1)S(1)} collective-permute-done((bf16[8,1280]{1,0:T(8,128)(2,1)S(1)}, bf16[8,1280]{1,0:T(8,128)(2,1)S(1)}, u32[]{:S(2)}, u32[]{:S(2)}) %collective-permute-start) | collective-permute-done | bytes 20512 | tf_op jit(solution)/shard_map/ppermute | solution.py:37
  5.8 1.9 %collective-permute-start.1 = (bf16[16,1280]{1,0:T(8,128)(2,1)S(1)}, bf16[16,1280]{1,0:T(8,128)(2,1)S(1)}, u32[]{:S(2)}, u32[]{:S(2)}) collective-permute-start(bf16[16,1280]{1,0:T(8,128)(2,1)S(1)} %pad_maximum_fusion.2), channel_id=1, source_target_pairs={{0,5},{1,4},{2,7},{3,6},{4,1},{5,0},{6,3},{7,2},{8,13},{9,12},{10,... | collective-permute-start | bytes 122888 | tf_op jit(solution)/shard_map/ppermute | solution.py:37
  7.6 1.7 %collective-permute-done.1 = bf16[16,1280]{1,0:T(8,128)(2,1)S(1)} collective-permute-done((bf16[16,1280]{1,0:T(8,128)(2,1)S(1)}, bf16[16,1280]{1,0:T(8,128)(2,1)S(1)}, u32[]{:S(2)}, u32[]{:S(2)}) %collective-permute-start.1) | collective-permute-done | bytes 40992 | tf_op jit(solution)/shard_map/ppermute | solution.py:37
  9.3 1.8 %collective-permute-start.2 = (bf16[32,1280]{1,0:T(8,128)(2,1)S(1)}, bf16[32,1280]{1,0:T(8,128)(2,1)S(1)}, u32[]{:S(2)}, u32[]{:S(2)}) collective-permute-start(bf16[32,1280]{1,0:T(8,128)(2,1)S(1)} %pad_maximum_fusion.1), channel_id=1, source_target_pairs={{0,3},{1,2},{2,1},{3,0},{4,7},{5,6},{6,5},{7,4},{8,11},{9,10},{10,... | collective-permute-start | bytes 245768 | tf_op jit(solution)/shard_map/ppermute | solution.py:37
  11.8 1.9 %collective-permute-done.2 = bf16[32,1280]{1,0:T(8,128)(2,1)S(1)} collective-permute-done((bf16[32,1280]{1,0:T(8,128)(2,1)S(1)}, bf16[32,1280]{1,0:T(8,128)(2,1)S(1)}, u32[]{:S(2)}, u32[]{:S(2)}) %collective-permute-start.2) | collective-permute-done | bytes 81952 | tf_op jit(solution)/shard_map/ppermute | solution.py:37
  13.7 0.0 copy-start
  13.7 0.3 %collective-permute-start.3 = (bf16[64,1280]{1,0:T(8,128)(2,1)S(1)}, bf16[64,1280]{1,0:T(8,128)(2,1)S(1)}, u32[]{:S(2)}, u32[]{:S(2)}) collective-permute-start(bf16[64,1280]{1,0:T(8,128)(2,1)S(1)} %pad_maximum_fusion.refs_2_), channel_id=1, source_target_pairs={{0,1},{1,0},{2,3},{3,2},{4,5},{5,4},{6,7},{7,6},{8,9},{9,8},{10,11... | collective-permute-start | bytes 491528 | tf_op jit(solution)/shard_map/ppermute | solution.py:37
  14.0 0.0 copy-start.1
  14.0 0.8 %copy-done.1 = s32[32]{0:T(128)S(1)} copy-done((s32[32]{0:T(128)S(1)}, s32[32]{0:T(128)}, u32[]{:S(2)}) %copy-start.1) | copy-done | bytes 152
  14.9 0.6 %stage.1.refs_1_ = f32[16,128]{1,0:T(8,128)S(1)} custom-call(s32[32]{0:T(128)S(1)} %copy-done.1, s32[1]{0:T(128)S(6)} %copy.6.valid_ref), custom_call_target="tpu_custom_call" | custom-call | flops 40000000000 | bytes 80000000 | tf_op jit(solution)/shard_map/stage/pallas_call | solution.py:178
  15.4 0.0 collective-permute-done.3.refs_3_
  15.4 0.1 copy-done
  15.6 3.2 %attend.1 = bf16[128,8192]{1,0:T(8,128)(2,1)} custom-call(bf16[128,12288]{1,0:T(8,128)(2,1)S(1)} %copy-done, f32[16,128]{1,0:T(8,128)S(1)} %stage.1.refs_1_, bf16[64,1280]{1,0:T(8,128)(2,1)S(1)} %pad_maximum_fusion.refs_2_, bf16[64,1280]{1,0:T(8,128)(2,1)S(1)} %collective-permute-done.3.refs_3_), custom_call_target="tpu_custom_call" | custom-call | tf_op jit(solution)/shard_map/attend/pallas_call | solution.py:156
  (3 shorter events, 0.0 us)
Async XLA Ops:
  0.7 5.0 %collective-permute-start = (bf16[8,1280]{1,0:T(8,128)(2,1)S(1)}, bf16[8,1280]{1,0:T(8,128)(2,1)S(1)}, u32[]{:S(2)}, u32[]{:S(2)}) collective-permute-start(bf16[8,1280]{1,0:T(8,128)(2,1)S(1)} %pad_maximum_fusion.3), channel_id=1, source_target_pairs={{0,9},{1,8},{2,11},{3,10},{4,13},{5,12},{6,15},{7,14},{8,1},{9,0},... | collective-permute-start | bytes 61448 | tf_op jit(solution)/shard_map/ppermute | solution.py:37
  5.8 3.5 %collective-permute-start.1 = (bf16[16,1280]{1,0:T(8,128)(2,1)S(1)}, bf16[16,1280]{1,0:T(8,128)(2,1)S(1)}, u32[]{:S(2)}, u32[]{:S(2)}) collective-permute-start(bf16[16,1280]{1,0:T(8,128)(2,1)S(1)} %pad_maximum_fusion.2), channel_id=1, source_target_pairs={{0,5},{1,4},{2,7},{3,6},{4,1},{5,0},{6,3},{7,2},{8,13},{9,12},{10,... | collective-permute-start | bytes 122888 | tf_op jit(solution)/shard_map/ppermute | solution.py:37
  9.3 4.3 %collective-permute-start.2 = (bf16[32,1280]{1,0:T(8,128)(2,1)S(1)}, bf16[32,1280]{1,0:T(8,128)(2,1)S(1)}, u32[]{:S(2)}, u32[]{:S(2)}) collective-permute-start(bf16[32,1280]{1,0:T(8,128)(2,1)S(1)} %pad_maximum_fusion.1), channel_id=1, source_target_pairs={{0,3},{1,2},{2,1},{3,0},{4,7},{5,6},{6,5},{7,4},{8,11},{9,10},{10,... | collective-permute-start | bytes 245768 | tf_op jit(solution)/shard_map/ppermute | solution.py:37
  13.7 1.9 %copy-start = (bf16[128,12288]{1,0:T(8,128)(2,1)S(1)}, bf16[128,12288]{1,0:T(8,128)(2,1)}, u32[]{:S(2)}) copy-start(bf16[128,12288]{1,0:T(8,128)(2,1)} %refs_0_.1) | copy-start | bytes 9437188
  13.7 1.7 %collective-permute-start.3 = (bf16[64,1280]{1,0:T(8,128)(2,1)S(1)}, bf16[64,1280]{1,0:T(8,128)(2,1)S(1)}, u32[]{:S(2)}, u32[]{:S(2)}) collective-permute-start(bf16[64,1280]{1,0:T(8,128)(2,1)S(1)} %pad_maximum_fusion.refs_2_), channel_id=1, source_target_pairs={{0,1},{1,0},{2,3},{3,2},{4,5},{5,4},{6,7},{7,6},{8,9},{9,8},{10,11... | collective-permute-start | bytes 491528 | tf_op jit(solution)/shard_map/ppermute | solution.py:37
  14.0 0.8 %copy-start.1 = (s32[32]{0:T(128)S(1)}, s32[32]{0:T(128)}, u32[]{:S(2)}) copy-start(s32[32]{0:T(128)} %limits_ref.1) | copy-start | bytes 388
